TPU v7x, 32 devices: a whole 2x2x4 slice. The times are simulated.
32 devices in a mesh: shot: 2 (over y), inline: 4 (over z), xline: 2 (over x), depth: 2 (over core).
Axes of the slice: x: 2, y: 2, z: 4, core: 2. Of those that a mesh axis runs over, the one named last changes fastest.
Arguments:
- forward_now: float32 [2, 32, 64, 256], P(None, ('shot', 'inline'), 'xline', 'depth'), parts along dimension 1, may hold values from -6 to 6
- forward_before: float32 [2, 32, 64, 256], P(None, ('shot', 'inline'), 'xline', 'depth'), parts along dimension 1, may hold values from -6 to 6
- adjoint_now: float32 [2, 32, 64, 256], P(None, ('shot', 'inline'), 'xline', 'depth'), parts along dimension 1, may hold values from -6 to 6
- adjoint_before: float32 [2, 32, 64, 256], P(None, ('shot', 'inline'), 'xline', 'depth'), parts along dimension 1, may hold values from -6 to 6
- courant: float32 [16, 64, 256], P('inline', 'xline', 'depth'), may hold values from 0.04 to 0.15
- thomsen_epsilon: float32 [16, 64, 256], P('inline', 'xline', 'depth'), may hold values from 0.2 to 0.4
- thomsen_delta: float32 [16, 64, 256], P('inline', 'xline', 'depth'), may hold values from 0 to 0.2
- tilt_class: int32 [16, 64, 256], P('inline', 'xline', 'depth'), may hold values from 0 to 15
- azimuth_class: int32 [16, 64, 256], P('inline', 'xline', 'depth'), may hold values from 0 to 31
- tilt_table: float32 [16], replicated, may hold values from -3.140625 to 3.140625
- azimuth_table: float32 [32], replicated, may hold values from -3.140625 to 3.140625
- source_cell: int32 [2], P('shot'), parts along dimension 0, may hold values from 0 to 262143
- wavelet: float32 [8], P('shot'), parts along dimension 0, may hold values from -6 to 6
- receiver_cells: int32 [4096], P('shot'), parts along dimension 0, may hold values from 0 to 262143
- receiver_data: float32 [4, 4096], P(None, 'shot'), parts along dimension 1, may hold values from -6 to 6
Outputs:
- forward_fields: float32 [2, 32, 64, 256], P(None, ('shot', 'inline'), 'xline', 'depth'), parts along dimension 1
- adjoint_fields: float32 [2, 32, 64, 256], P(None, ('shot', 'inline'), 'xline', 'depth'), parts along dimension 1
- migrated_image: float32 [32, 64, 256], P(('shot', 'inline'), 'xline', 'depth'), parts along dimension 0
- traces: float32 [4, 4096], P(None, 'shot'), parts along dimension 1
There are 2 independent parts, one for each index of `shot`. A program takes and returns all parts, laid end to end along the dimension named above; an argument that names none is the same for every part. Nothing has to cross between parts.
All inputs are finite; a program needn't handle non-finite values.
Results may differ from a plain program's by a relative error of at most 0.00002.
Values sent between devices are 32-bit elements; how exact they have to be, the bound alone decides.
A program may use at most 128 MiB of HBM per device.

v0:
```python
import jax
import jax.numpy as jnp
from jax import lax
from jax.sharding import PartitionSpec as P

STEPS = 4


def with_halo(value, sides, width):
    for axis, dim in sides:
        size, length = (lax.axis_size(axis), value.shape[dim])
        up = [(i, (i + 1) % size) for i in range(size - 1)]
        down = [(j, i) for i, j in up]
        last = lax.slice_in_dim(value, length - width, length, axis=dim)
        initial = lax.slice_in_dim(value, 0, width, axis=dim)
        before = lax.ppermute(last, axis, up)
        after = lax.ppermute(initial, axis, down)
        value = jnp.concatenate([before, value, after], axis=dim)
    return value


def differences(padded):
    centre = padded[..., 1:-1, 1:-1, 1:-1]
    inline_inline = padded[..., 2:, 1:-1, 1:-1] + padded[..., :-2, 1:-1, 1:-1] - 2.0 * centre
    xline_xline = padded[..., 1:-1, 2:, 1:-1] + padded[..., 1:-1, :-2, 1:-1] - 2.0 * centre
    depth_depth = padded[..., 1:-1, 1:-1, 2:] + padded[..., 1:-1, 1:-1, :-2] - 2.0 * centre
    inline_xline = 0.25 * (
        padded[..., 2:, 2:, 1:-1]
        - padded[..., 2:, :-2, 1:-1]
        - padded[..., :-2, 2:, 1:-1]
        + padded[..., :-2, :-2, 1:-1]
    )
    inline_depth = 0.25 * (
        padded[..., 2:, 1:-1, 2:]
        - padded[..., 2:, 1:-1, :-2]
        - padded[..., :-2, 1:-1, 2:]
        + padded[..., :-2, 1:-1, :-2]
    )
    xline_depth = 0.25 * (
        padded[..., 1:-1, 2:, 2:]
        - padded[..., 1:-1, 2:, :-2]
        - padded[..., 1:-1, :-2, 2:]
        + padded[..., 1:-1, :-2, :-2]
    )
    return (
        centre,
        inline_inline,
        xline_xline,
        depth_depth,
        inline_xline,
        inline_depth,
        xline_depth,
    )


def advance(padded, before, factors):
    centre, inline_inline, xline_xline, depth_depth, inline_xline, inline_depth, xline_depth = (
        differences(padded)
    )
    axial_part = (
        factors[3] * inline_inline
        + factors[4] * xline_xline
        + factors[5] * depth_depth
        + factors[6] * inline_xline
        + factors[7] * inline_depth
        + factors[8] * xline_depth
    )
    plane_part = (inline_inline + xline_xline + depth_depth)[0::2] - axial_part[0::2]
    pressure = (
        2.0 * centre[0::2] - before[0::2] + factors[0] * plane_part + factors[2] * axial_part[1::2]
    )
    auxiliary = (
        2.0 * centre[1::2] - before[1::2] + factors[1] * plane_part + factors[2] * axial_part[1::2]
    )
    return jnp.stack([pressure[0], auxiliary[0], pressure[1], auxiliary[1]])


def lookup(classes, table_rows):
    class_range = jnp.arange(table_rows.shape[1], dtype=jnp.int32)
    matches = classes[None] == class_range[:, None, None, None]
    return [
        jnp.sum(jnp.where(matches, entry_row[:, None, None, None], 0.0), axis=0)
        for entry_row in table_rows
    ]


def coefficients(
    courant, thomsen_epsilon, thomsen_delta, tilt_class, azimuth_class, tilt_table, azimuth_table
):
    tilt_sine, tilt_cosine = lookup(
        tilt_class, jnp.stack([jnp.sin(tilt_table), jnp.cos(tilt_table)])
    )
    azimuth_cosine, azimuth_sine = lookup(
        azimuth_class, jnp.stack([jnp.cos(azimuth_table), jnp.sin(azimuth_table)])
    )
    axis_first = tilt_sine * azimuth_cosine
    axis_second = tilt_sine * azimuth_sine
    return jnp.stack(
        [
            courant * (1.0 + 2.0 * thomsen_epsilon),
            courant * (1.0 + 2.0 * thomsen_delta),
            courant,
            axis_first * axis_first,
            axis_second * axis_second,
            tilt_cosine * tilt_cosine,
            2.0 * axis_first * axis_second,
            2.0 * axis_first * tilt_cosine,
            2.0 * axis_second * tilt_cosine,
        ]
    )


def locate(cells, anchor, extent, layout):
    inline_at = cells // (layout[0] * layout[1]) - anchor[0]
    xline_at = cells // layout[1] % layout[0] - anchor[1]
    depth_at = cells % layout[1] - anchor[2]
    inside = (
        (inline_at >= 0)
        & (inline_at < extent[0])
        & (xline_at >= 0)
        & (xline_at < extent[1])
        & (depth_at >= 0)
        & (depth_at < extent[2])
    )
    volume = extent[0] * extent[1] * extent[2]
    flat_index = jnp.where(
        inside, (inline_at * extent[1] + xline_at) * extent[2] + depth_at, volume
    )
    return (flat_index, inside)


def deposit(values, flat_index, extent):
    volume = extent[0] * extent[1] * extent[2]
    return jnp.zeros((volume + 1,), jnp.float32).at[flat_index].add(values)[:volume].reshape(extent)


def sample(field, flat_index, inside):
    volume = field.size
    picked = field.reshape(-1)[jnp.minimum(flat_index, volume - 1)]
    return jnp.where(inside, picked, 0.0)


def per_device(
    forward_now,
    forward_before,
    adjoint_now,
    adjoint_before,
    courant,
    thomsen_epsilon,
    thomsen_delta,
    tilt_class,
    azimuth_class,
    tilt_table,
    azimuth_table,
    source_cell,
    wavelet,
    receiver_cells,
    receiver_data,
):
    inline_cells, xline_cells, depth_cells = courant.shape
    layout = (xline_cells * lax.axis_size("xline"), depth_cells * lax.axis_size("depth"))
    anchor = (
        lax.axis_index("inline") * inline_cells,
        lax.axis_index("xline") * xline_cells,
        lax.axis_index("depth") * depth_cells,
    )
    own_extent = (inline_cells, xline_cells, depth_cells)
    own_index, own_inside = locate(receiver_cells, anchor, own_extent, layout)
    current = jnp.concatenate([forward_now, adjoint_now])
    previous = jnp.concatenate([forward_before, adjoint_before])
    image_sum = jnp.zeros(own_extent, jnp.float32)
    records = []
    factors = coefficients(
        courant,
        thomsen_epsilon,
        thomsen_delta,
        tilt_class,
        azimuth_class,
        tilt_table,
        azimuth_table,
    )
    for moment in range(STEPS):
        padded = with_halo(current, (("inline", 1), ("xline", 2), ("depth", 3)), 1)
        shifted = (anchor[0] - 0, anchor[1] - 0, anchor[2] - 0)
        source_index, source_inside = locate(source_cell, shifted, own_extent, layout)
        receiver_index, receiver_inside = locate(receiver_cells, shifted, own_extent, layout)
        source_term = deposit(
            jnp.broadcast_to(wavelet[moment], source_cell.shape), source_index, own_extent
        )
        receiver_term = deposit(receiver_data[moment], receiver_index, own_extent)
        updated = advance(padded, previous, factors) + jnp.stack(
            [source_term, source_term, receiver_term, receiver_term]
        )
        image_sum = image_sum + updated[0] * updated[2] + updated[1] * updated[3]
        records.append(sample(updated[0], own_index, own_inside))
        previous, current = (current, updated)
    traces = lax.psum(jnp.stack(records), ("inline", "xline", "depth"))
    return (current[:2], current[2:], image_sum, traces)


def solution(mesh):
    return jax.shard_map(
        per_device,
        mesh=mesh,
        in_specs=(
            P(None, ("shot", "inline"), "xline", "depth"),
            P(None, ("shot", "inline"), "xline", "depth"),
            P(None, ("shot", "inline"), "xline", "depth"),
            P(None, ("shot", "inline"), "xline", "depth"),
            P("inline", "xline", "depth"),
            P("inline", "xline", "depth"),
            P("inline", "xline", "depth"),
            P("inline", "xline", "depth"),
            P("inline", "xline", "depth"),
            P(),
            P(),
            P("shot"),
            P("shot"),
            P("shot"),
            P(None, "shot"),
        ),
        out_specs=(
            P(None, ("shot", "inline"), "xline", "depth"),
            P(None, ("shot", "inline"), "xline", "depth"),
            P(("shot", "inline"), "xline", "depth"),
            P(None, "shot"),
        ),
        check_vma=False,
    )
```

profile of v0, /device:TPU:0, one launch (start us, length us, event | category | flops | bytes accessed | tf_op | source)
XLA Modules:
  0.0 266.9 jit_solution(2049684719237770810)
XLA Ops:
  2.7 1.4 collective-permute-start
  4.1 5.6 %collective-permute-start.1 = (f32[4,1,32,128]{3,2,1,0:T(8,128)S(1)}, f32[4,1,32,128]{3,2,1,0:T(8,128)S(1)}, u32[]{:S(2)}, u32[]{:S(2)}) collective-permute-start(f32[4,1,32,128]{3,2,1,0:T(8,128)S(1)} %get-tuple-element.111), channel_id=1, source_target_pairs={{0,4},{4,8},{8,12},{1,5},{5,9},{9,13},{2,6},{6,10},{10,14},{3,7},{... | collective-permute-start | bytes 196616 | tf_op jit(solution)/shard_map/ppermute | solution.py:16
  14.2 4.5 %collective-permute-start.3 = (f32[4,6,1,128]{3,2,1,0:T(1,128)S(1)}, f32[4,6,1,128]{3,2,1,0:T(1,128)S(1)}, u32[]{:S(2)}, u32[]{:S(2)}) collective-permute-start(f32[4,6,1,128]{3,2,1,0:T(1,128)S(1)} %get-tuple-element.97), channel_id=1, source_target_pairs={{0,2},{1,3},{4,6},{5,7},{8,10},{9,11},{12,14},{13,15},{16,18},{17,... | collective-permute-start | bytes 36872 | tf_op jit(solution)/shard_map/ppermute | solution.py:16
  18.8 1.4 select_dynamic-update-slice_fusion.3
  20.2 13.9 %scatter_custom_fusion = f32[16385]{0:T(1024)S(1)} fusion(s32[2048]{0:T(1024)S(1)} %compare_select_fusion.1, f32[2048]{0:T(1024)S(1)} %bitcast.45, f32[]{:T(128)} %constant.257.clone.1), kind=kCustom, calls=%fused_computation.177 | custom fusion | flops 2048 | bytes 65544 | tf_op jit(solution)/shard_map/scatter-add | solution.py:134
  36.0 3.1 %collective-permute-start.5 = (f32[4,6,34,1]{3,2,1,0:T(8,128)S(1)}, f32[4,6,34,1]{3,2,1,0:T(8,128)S(1)}, u32[]{:S(2)}, u32[]{:S(2)}) collective-permute-start(f32[4,6,34,1]{3,2,1,0:T(8,128)S(1)} %get-tuple-element.74), channel_id=1, source_target_pairs={{0,1},{2,3},{4,5},{6,7},{8,9},{10,11},{12,13},{14,15},{16,17},{18,... | collective-permute-start | bytes 9800 | tf_op jit(solution)/shard_map/ppermute | solution.py:16
  39.2 1.4 collective-permute-done.5
  44.0 4.5 %collective-permute-start.7 = (f32[4,1,32,128]{3,2,1,0:T(8,128)S(1)}, f32[4,1,32,128]{3,2,1,0:T(8,128)S(1)}, u32[]{:S(2)}, u32[]{:S(2)}) collective-permute-start(f32[4,1,32,128]{3,2,1,0:T(8,128)S(1)} %get-tuple-element.109), channel_id=1, source_target_pairs={{0,4},{4,8},{8,12},{1,5},{5,9},{9,13},{2,6},{6,10},{10,14},{3,7},{... | collective-permute-start | bytes 196616 | tf_op jit(solution)/shard_map/ppermute | solution.py:16
  49.1 1.3 collective-permute-done.7
  51.7 4.5 %collective-permute-start.9 = (f32[4,6,1,128]{3,2,1,0:T(1,128)S(1)}, f32[4,6,1,128]{3,2,1,0:T(1,128)S(1)}, u32[]{:S(2)}, u32[]{:S(2)}) collective-permute-start(f32[4,6,1,128]{3,2,1,0:T(1,128)S(1)} %get-tuple-element.93), channel_id=1, source_target_pairs={{0,2},{1,3},{4,6},{5,7},{8,10},{9,11},{12,14},{13,15},{16,18},{17,... | collective-permute-start | bytes 36872 | tf_op jit(solution)/shard_map/ppermute | solution.py:16
  56.3 1.5 select_dynamic-update-slice_fusion.2
  57.8 13.9 %scatter_custom_fusion.1 = f32[16385]{0:T(1024)S(1)} fusion(s32[2048]{0:T(1024)S(1)} %compare_select_fusion.1, f32[2048]{0:T(1024)S(1)} %bitcast.44, f32[]{:T(128)} %constant.257.clone.1), kind=kCustom, calls=%fused_computation.175 | custom fusion | flops 2048 | bytes 65544 | tf_op jit(solution)/shard_map/scatter-add | solution.py:134
  73.6 3.1 %collective-permute-start.11 = (f32[4,6,34,1]{3,2,1,0:T(8,128)S(1)}, f32[4,6,34,1]{3,2,1,0:T(8,128)S(1)}, u32[]{:S(2)}, u32[]{:S(2)}) collective-permute-start(f32[4,6,34,1]{3,2,1,0:T(8,128)S(1)} %get-tuple-element.72), channel_id=1, source_target_pairs={{0,1},{2,3},{4,5},{6,7},{8,9},{10,11},{12,13},{14,15},{16,17},{18,... | collective-permute-start | bytes 9800 | tf_op jit(solution)/shard_map/ppermute | solution.py:16
  76.8 1.4 collective-permute-done.11
  81.5 4.8 %collective-permute-start.13 = (f32[4,1,32,128]{3,2,1,0:T(8,128)S(1)}, f32[4,1,32,128]{3,2,1,0:T(8,128)S(1)}, u32[]{:S(2)}, u32[]{:S(2)}) collective-permute-start(f32[4,1,32,128]{3,2,1,0:T(8,128)S(1)} %get-tuple-element.107), channel_id=1, source_target_pairs={{0,4},{4,8},{8,12},{1,5},{5,9},{9,13},{2,6},{6,10},{10,14},{3,7},{... | collective-permute-start | bytes 196616 | tf_op jit(solution)/shard_map/ppermute | solution.py:16
  88.2 1.3 collective-permute-start.14
  89.5 4.5 %collective-permute-start.15 = (f32[4,6,1,128]{3,2,1,0:T(1,128)S(1)}, f32[4,6,1,128]{3,2,1,0:T(1,128)S(1)}, u32[]{:S(2)}, u32[]{:S(2)}) collective-permute-start(f32[4,6,1,128]{3,2,1,0:T(1,128)S(1)} %get-tuple-element.89), channel_id=1, source_target_pairs={{0,2},{1,3},{4,6},{5,7},{8,10},{9,11},{12,14},{13,15},{16,18},{17,... | collective-permute-start | bytes 36872 | tf_op jit(solution)/shard_map/ppermute | solution.py:16
  94.1 1.5 select_dynamic-update-slice_fusion.1
  95.6 13.9 %scatter_custom_fusion.2 = f32[16385]{0:T(1024)S(1)} fusion(s32[2048]{0:T(1024)S(1)} %compare_select_fusion.1, f32[2048]{0:T(1024)S(1)} %bitcast.43, f32[]{:T(128)} %constant.257.clone.1), kind=kCustom, calls=%fused_computation.173 | custom fusion | flops 2048 | bytes 65544 | tf_op jit(solution)/shard_map/scatter-add | solution.py:134
  111.4 3.3 %collective-permute-start.17 = (f32[4,6,34,1]{3,2,1,0:T(8,128)S(1)}, f32[4,6,34,1]{3,2,1,0:T(8,128)S(1)}, u32[]{:S(2)}, u32[]{:S(2)}) collective-permute-start(f32[4,6,34,1]{3,2,1,0:T(8,128)S(1)} %get-tuple-element.70), channel_id=1, source_target_pairs={{0,1},{2,3},{4,5},{6,7},{8,9},{10,11},{12,13},{14,15},{16,17},{18,... | collective-permute-start | bytes 9800 | tf_op jit(solution)/shard_map/ppermute | solution.py:16
  118.0 1.3 collective-permute-start.18
  119.3 4.9 %collective-permute-start.19 = (f32[4,1,32,128]{3,2,1,0:T(8,128)S(1)}, f32[4,1,32,128]{3,2,1,0:T(8,128)S(1)}, u32[]{:S(2)}, u32[]{:S(2)}) collective-permute-start(f32[4,1,32,128]{3,2,1,0:T(8,128)S(1)} %get-tuple-element.105), channel_id=1, source_target_pairs={{0,4},{4,8},{8,12},{1,5},{5,9},{9,13},{2,6},{6,10},{10,14},{3,7},{... | collective-permute-start | bytes 196616 | tf_op jit(solution)/shard_map/ppermute | solution.py:16
  127.4 4.5 %collective-permute-start.21 = (f32[4,6,1,128]{3,2,1,0:T(1,128)S(1)}, f32[4,6,1,128]{3,2,1,0:T(1,128)S(1)}, u32[]{:S(2)}, u32[]{:S(2)}) collective-permute-start(f32[4,6,1,128]{3,2,1,0:T(1,128)S(1)} %get-tuple-element.85), channel_id=1, source_target_pairs={{0,2},{1,3},{4,6},{5,7},{8,10},{9,11},{12,14},{13,15},{16,18},{17,... | collective-permute-start | bytes 36872 | tf_op jit(solution)/shard_map/ppermute | solution.py:16
  132.0 1.5 select_dynamic-update-slice_fusion
  133.4 13.9 %scatter_custom_fusion.3 = f32[16385]{0:T(1024)S(1)} fusion(s32[2048]{0:T(1024)S(1)} %compare_select_fusion.1, f32[2048]{0:T(1024)S(1)} %bitcast.42, f32[]{:T(128)} %constant.257.clone.1), kind=kCustom, calls=%fused_computation.171 | custom fusion | flops 2048 | bytes 65544 | tf_op jit(solution)/shard_map/scatter-add | solution.py:134
  149.3 3.1 %collective-permute-start.23 = (f32[4,6,34,1]{3,2,1,0:T(8,128)S(1)}, f32[4,6,34,1]{3,2,1,0:T(8,128)S(1)}, u32[]{:S(2)}, u32[]{:S(2)}) collective-permute-start(f32[4,6,34,1]{3,2,1,0:T(8,128)S(1)} %get-tuple-element.68), channel_id=1, source_target_pairs={{0,1},{2,3},{4,5},{6,7},{8,9},{10,11},{12,13},{14,15},{16,17},{18,... | collective-permute-start | bytes 9800 | tf_op jit(solution)/shard_map/ppermute | solution.py:16
  152.5 1.4 collective-permute-done.23
  157.4 11.8 %gather_fusion = f32[2048]{0:T(1024)S(1)} fusion(f32[16384]{0:T(1024)S(1)} %bitcast.28, s32[2048]{0:T(1024)S(1)} %get-tuple-element.56), kind=kCustom, calls=%fused_computation | custom fusion | bytes 24576 | tf_op jit(solution)/shard_map/gather | solution.py:139
  169.2 11.8 %gather_fusion.2 = f32[2048]{0:T(1024)S(1)} fusion(f32[16384]{0:T(1024)S(1)} %bitcast.27, s32[2048]{0:T(1024)S(1)} %get-tuple-element.56), kind=kCustom, calls=%fused_computation.2 | custom fusion | bytes 24576 | tf_op jit(solution)/shard_map/gather | solution.py:139
  181.0 11.8 %gather_fusion.1 = f32[2048]{0:T(1024)S(1)} fusion(f32[16384]{0:T(1024)S(1)} %bitcast.26, s32[2048]{0:T(1024)S(1)} %get-tuple-element.56), kind=kCustom, calls=%fused_computation.1 | custom fusion | bytes 24576 | tf_op jit(solution)/shard_map/gather | solution.py:139
  192.8 11.8 %gather_fusion.3 = f32[2048]{0:T(1024)S(1)} fusion(f32[16384]{0:T(1024)S(1)} %bitcast.29, s32[2048]{0:T(1024)S(1)} %get-tuple-element.56), kind=kCustom, calls=%fused_computation.3 | custom fusion | bytes 24576 | tf_op jit(solution)/shard_map/gather | solution.py:139
  204.6 62.3 %psum.7 = f32[4,2048]{1,0:T(4,128)} all-reduce(f32[4,2048]{1,0:T(4,128)S(1)} %pad_maximum_fusion.20), channel_id=1, replica_groups=mesh['shot'=2,'inline'=4,'xline'=2,'depth'=2] {'inline','xline','depth'}, use_global_device_ids=true, to_apply=%region_8.9 | all-reduce | flops 8192 | bytes 65536 | tf_op jit(solution)/shard_map/psum | solution.py:197
  (143 shorter events, 33.4 us)
Async XLA Ops:
  0.7 10.1 %copy-start.11 = (f32[4,2048]{1,0:T(4,128)S(1)}, f32[4,2048]{1,0:T(4,128)}, u32[]{:S(2)}) copy-start(f32[4,2048]{1,0:T(4,128)} %param.37) | copy-start | bytes 98308
  0.7 10.8 %copy-start.7 = (s32[4,32,128]{2,1,0:T(8,128)S(1)}, s32[4,32,128]{2,1,0:T(8,128)}, u32[]{:S(2)}) copy-start(s32[4,32,128]{2,1,0:T(8,128)} %param.30) | copy-start | bytes 196612
  0.7 11.1 %copy-start.8 = (s32[4,32,128]{2,1,0:T(8,128)S(1)}, s32[4,32,128]{2,1,0:T(8,128)}, u32[]{:S(2)}) copy-start(s32[4,32,128]{2,1,0:T(8,128)} %param.31) | copy-start | bytes 196612
  0.7 11.5 %copy-start.1 = (f32[4,32,128]{2,1,0:T(8,128)S(1)}, f32[4,32,128]{2,1,0:T(8,128)}, u32[]{:S(2)}) copy-start(f32[4,32,128]{2,1,0:T(8,128)} %param.27) | copy-start | bytes 196612
  0.7 11.5 %copy-start.9 = (f32[4,32,128]{2,1,0:T(8,128)S(1)}, f32[4,32,128]{2,1,0:T(8,128)}, u32[]{:S(2)}) copy-start(f32[4,32,128]{2,1,0:T(8,128)} %param.28) | copy-start | bytes 196612
  0.7 11.5 %copy-start.10 = (f32[4,32,128]{2,1,0:T(8,128)S(1)}, f32[4,32,128]{2,1,0:T(8,128)}, u32[]{:S(2)}) copy-start(f32[4,32,128]{2,1,0:T(8,128)} %param.29) | copy-start | bytes 196612
  2.7 10.2 %copy-start.6 = (f32[2,4,32,128]{3,2,1,0:T(8,128)S(1)}, f32[2,4,32,128]{3,2,1,0:T(8,128)}, u32[]{:S(2)}) copy-start(f32[2,4,32,128]{3,2,1,0:T(8,128)} %param.26) | copy-start | bytes 393220
  2.7 10.2 %collective-permute-start = (f32[4,1,32,128]{3,2,1,0:T(8,128)S(1)}, f32[4,1,32,128]{3,2,1,0:T(8,128)S(1)}, u32[]{:S(2)}, u32[]{:S(2)}) collective-permute-start(f32[4,1,32,128]{3,2,1,0:T(8,128)S(1)} %get-tuple-element.112), channel_id=1, source_target_pairs={{4,0},{8,4},{12,8},{5,1},{9,5},{13,9},{6,2},{10,6},{14,10},{7,3},{... | collective-permute-start | bytes 196616 | tf_op jit(solution)/shard_map/ppermute | solution.py:17
  4.1 8.8 %collective-permute-start.1 = (f32[4,1,32,128]{3,2,1,0:T(8,128)S(1)}, f32[4,1,32,128]{3,2,1,0:T(8,128)S(1)}, u32[]{:S(2)}, u32[]{:S(2)}) collective-permute-start(f32[4,1,32,128]{3,2,1,0:T(8,128)S(1)} %get-tuple-element.111), channel_id=1, source_target_pairs={{0,4},{4,8},{8,12},{1,5},{5,9},{9,13},{2,6},{6,10},{10,14},{3,7},{... | collective-permute-start | bytes 196616 | tf_op jit(solution)/shard_map/ppermute | solution.py:16
  12.9 21.2 %collective-permute-start.2 = (f32[4,6,1,128]{3,2,1,0:T(1,128)S(1)}, f32[4,6,1,128]{3,2,1,0:T(1,128)S(1)}, u32[]{:S(2)}, u32[]{:S(2)}) collective-permute-start(f32[4,6,1,128]{3,2,1,0:T(1,128)S(1)} %get-tuple-element.98), channel_id=1, source_target_pairs={{2,0},{3,1},{6,4},{7,5},{10,8},{11,9},{14,12},{15,13},{18,16},{19,... | collective-permute-start | bytes 36872 | tf_op jit(solution)/shard_map/ppermute | solution.py:17
  14.2 19.9 %collective-permute-start.3 = (f32[4,6,1,128]{3,2,1,0:T(1,128)S(1)}, f32[4,6,1,128]{3,2,1,0:T(1,128)S(1)}, u32[]{:S(2)}, u32[]{:S(2)}) collective-permute-start(f32[4,6,1,128]{3,2,1,0:T(1,128)S(1)} %get-tuple-element.97), channel_id=1, source_target_pairs={{0,2},{1,3},{4,6},{5,7},{8,10},{9,11},{12,14},{13,15},{16,18},{17,... | collective-permute-start | bytes 36872 | tf_op jit(solution)/shard_map/ppermute | solution.py:16
  34.7 4.5 %collective-permute-start.4 = (f32[4,6,34,1]{3,2,1,0:T(8,128)S(1)}, f32[4,6,34,1]{3,2,1,0:T(8,128)S(1)}, u32[]{:S(2)}, u32[]{:S(2)}) collective-permute-start(f32[4,6,34,1]{3,2,1,0:T(8,128)S(1)} %get-tuple-element.73), channel_id=1, source_target_pairs={{1,0},{3,2},{5,4},{7,6},{9,8},{11,10},{13,12},{15,14},{17,16},{19,... | collective-permute-start | bytes 9800 | tf_op jit(solution)/shard_map/ppermute | solution.py:17
  36.0 4.5 %collective-permute-start.5 = (f32[4,6,34,1]{3,2,1,0:T(8,128)S(1)}, f32[4,6,34,1]{3,2,1,0:T(8,128)S(1)}, u32[]{:S(2)}, u32[]{:S(2)}) collective-permute-start(f32[4,6,34,1]{3,2,1,0:T(8,128)S(1)} %get-tuple-element.74), channel_id=1, source_target_pairs={{0,1},{2,3},{4,5},{6,7},{8,9},{10,11},{12,13},{14,15},{16,17},{18,... | collective-permute-start | bytes 9800 | tf_op jit(solution)/shard_map/ppermute | solution.py:16
  42.7 6.4 %collective-permute-start.6 = (f32[4,1,32,128]{3,2,1,0:T(8,128)S(1)}, f32[4,1,32,128]{3,2,1,0:T(8,128)S(1)}, u32[]{:S(2)}, u32[]{:S(2)}) collective-permute-start(f32[4,1,32,128]{3,2,1,0:T(8,128)S(1)} %get-tuple-element.110), channel_id=1, source_target_pairs={{4,0},{8,4},{12,8},{5,1},{9,5},{13,9},{6,2},{10,6},{14,10},{7,3},{... | collective-permute-start | bytes 196616 | tf_op jit(solution)/shard_map/ppermute | solution.py:17
  44.0 6.4 %collective-permute-start.7 = (f32[4,1,32,128]{3,2,1,0:T(8,128)S(1)}, f32[4,1,32,128]{3,2,1,0:T(8,128)S(1)}, u32[]{:S(2)}, u32[]{:S(2)}) collective-permute-start(f32[4,1,32,128]{3,2,1,0:T(8,128)S(1)} %get-tuple-element.109), channel_id=1, source_target_pairs={{0,4},{4,8},{8,12},{1,5},{5,9},{9,13},{2,6},{6,10},{10,14},{3,7},{... | collective-permute-start | bytes 196616 | tf_op jit(solution)/shard_map/ppermute | solution.py:16
  50.4 21.3 %collective-permute-start.8 = (f32[4,6,1,128]{3,2,1,0:T(1,128)S(1)}, f32[4,6,1,128]{3,2,1,0:T(1,128)S(1)}, u32[]{:S(2)}, u32[]{:S(2)}) collective-permute-start(f32[4,6,1,128]{3,2,1,0:T(1,128)S(1)} %get-tuple-element.94), channel_id=1, source_target_pairs={{2,0},{3,1},{6,4},{7,5},{10,8},{11,9},{14,12},{15,13},{18,16},{19,... | collective-permute-start | bytes 36872 | tf_op jit(solution)/shard_map/ppermute | solution.py:17
  51.7 20.0 %collective-permute-start.9 = (f32[4,6,1,128]{3,2,1,0:T(1,128)S(1)}, f32[4,6,1,128]{3,2,1,0:T(1,128)S(1)}, u32[]{:S(2)}, u32[]{:S(2)}) collective-permute-start(f32[4,6,1,128]{3,2,1,0:T(1,128)S(1)} %get-tuple-element.93), channel_id=1, source_target_pairs={{0,2},{1,3},{4,6},{5,7},{8,10},{9,11},{12,14},{13,15},{16,18},{17,... | collective-permute-start | bytes 36872 | tf_op jit(solution)/shard_map/ppermute | solution.py:16
  72.3 4.5 %collective-permute-start.10 = (f32[4,6,34,1]{3,2,1,0:T(8,128)S(1)}, f32[4,6,34,1]{3,2,1,0:T(8,128)S(1)}, u32[]{:S(2)}, u32[]{:S(2)}) collective-permute-start(f32[4,6,34,1]{3,2,1,0:T(8,128)S(1)} %get-tuple-element.71), channel_id=1, source_target_pairs={{1,0},{3,2},{5,4},{7,6},{9,8},{11,10},{13,12},{15,14},{17,16},{19,... | collective-permute-start | bytes 9800 | tf_op jit(solution)/shard_map/ppermute | solution.py:17
  73.6 4.5 %collective-permute-start.11 = (f32[4,6,34,1]{3,2,1,0:T(8,128)S(1)}, f32[4,6,34,1]{3,2,1,0:T(8,128)S(1)}, u32[]{:S(2)}, u32[]{:S(2)}) collective-permute-start(f32[4,6,34,1]{3,2,1,0:T(8,128)S(1)} %get-tuple-element.72), channel_id=1, source_target_pairs={{0,1},{2,3},{4,5},{6,7},{8,9},{10,11},{12,13},{14,15},{16,17},{18,... | collective-permute-start | bytes 9800 | tf_op jit(solution)/shard_map/ppermute | solution.py:16
  80.2 6.8 %collective-permute-start.12 = (f32[4,1,32,128]{3,2,1,0:T(8,128)S(1)}, f32[4,1,32,128]{3,2,1,0:T(8,128)S(1)}, u32[]{:S(2)}, u32[]{:S(2)}) collective-permute-start(f32[4,1,32,128]{3,2,1,0:T(8,128)S(1)} %get-tuple-element.108), channel_id=1, source_target_pairs={{4,0},{8,4},{12,8},{5,1},{9,5},{13,9},{6,2},{10,6},{14,10},{7,3},{... | collective-permute-start | bytes 196616 | tf_op jit(solution)/shard_map/ppermute | solution.py:17
  81.5 6.7 %collective-permute-start.13 = (f32[4,1,32,128]{3,2,1,0:T(8,128)S(1)}, f32[4,1,32,128]{3,2,1,0:T(8,128)S(1)}, u32[]{:S(2)}, u32[]{:S(2)}) collective-permute-start(f32[4,1,32,128]{3,2,1,0:T(8,128)S(1)} %get-tuple-element.107), channel_id=1, source_target_pairs={{0,4},{4,8},{8,12},{1,5},{5,9},{9,13},{2,6},{6,10},{10,14},{3,7},{... | collective-permute-start | bytes 196616 | tf_op jit(solution)/shard_map/ppermute | solution.py:16
  88.2 21.3 %collective-permute-start.14 = (f32[4,6,1,128]{3,2,1,0:T(1,128)S(1)}, f32[4,6,1,128]{3,2,1,0:T(1,128)S(1)}, u32[]{:S(2)}, u32[]{:S(2)}) collective-permute-start(f32[4,6,1,128]{3,2,1,0:T(1,128)S(1)} %get-tuple-element.90), channel_id=1, source_target_pairs={{2,0},{3,1},{6,4},{7,5},{10,8},{11,9},{14,12},{15,13},{18,16},{19,... | collective-permute-start | bytes 36872 | tf_op jit(solution)/shard_map/ppermute | solution.py:17
  89.5 20.0 %collective-permute-start.15 = (f32[4,6,1,128]{3,2,1,0:T(1,128)S(1)}, f32[4,6,1,128]{3,2,1,0:T(1,128)S(1)}, u32[]{:S(2)}, u32[]{:S(2)}) collective-permute-start(f32[4,6,1,128]{3,2,1,0:T(1,128)S(1)} %get-tuple-element.89), channel_id=1, source_target_pairs={{0,2},{1,3},{4,6},{5,7},{8,10},{9,11},{12,14},{13,15},{16,18},{17,... | collective-permute-start | bytes 36872 | tf_op jit(solution)/shard_map/ppermute | solution.py:16
  110.1 4.6 %collective-permute-start.16 = (f32[4,6,34,1]{3,2,1,0:T(8,128)S(1)}, f32[4,6,34,1]{3,2,1,0:T(8,128)S(1)}, u32[]{:S(2)}, u32[]{:S(2)}) collective-permute-start(f32[4,6,34,1]{3,2,1,0:T(8,128)S(1)} %get-tuple-element.69), channel_id=1, source_target_pairs={{1,0},{3,2},{5,4},{7,6},{9,8},{11,10},{13,12},{15,14},{17,16},{19,... | collective-permute-start | bytes 9800 | tf_op jit(solution)/shard_map/ppermute | solution.py:17
  111.4 4.5 %collective-permute-start.17 = (f32[4,6,34,1]{3,2,1,0:T(8,128)S(1)}, f32[4,6,34,1]{3,2,1,0:T(8,128)S(1)}, u32[]{:S(2)}, u32[]{:S(2)}) collective-permute-start(f32[4,6,34,1]{3,2,1,0:T(8,128)S(1)} %get-tuple-element.70), channel_id=1, source_target_pairs={{0,1},{2,3},{4,5},{6,7},{8,9},{10,11},{12,13},{14,15},{16,17},{18,... | collective-permute-start | bytes 9800 | tf_op jit(solution)/shard_map/ppermute | solution.py:16
  118.0 6.9 %collective-permute-start.18 = (f32[4,1,32,128]{3,2,1,0:T(8,128)S(1)}, f32[4,1,32,128]{3,2,1,0:T(8,128)S(1)}, u32[]{:S(2)}, u32[]{:S(2)}) collective-permute-start(f32[4,1,32,128]{3,2,1,0:T(8,128)S(1)} %get-tuple-element.106), channel_id=1, source_target_pairs={{4,0},{8,4},{12,8},{5,1},{9,5},{13,9},{6,2},{10,6},{14,10},{7,3},{... | collective-permute-start | bytes 196616 | tf_op jit(solution)/shard_map/ppermute | solution.py:17
  119.3 6.8 %collective-permute-start.19 = (f32[4,1,32,128]{3,2,1,0:T(8,128)S(1)}, f32[4,1,32,128]{3,2,1,0:T(8,128)S(1)}, u32[]{:S(2)}, u32[]{:S(2)}) collective-permute-start(f32[4,1,32,128]{3,2,1,0:T(8,128)S(1)} %get-tuple-element.105), channel_id=1, source_target_pairs={{0,4},{4,8},{8,12},{1,5},{5,9},{9,13},{2,6},{6,10},{10,14},{3,7},{... | collective-permute-start | bytes 196616 | tf_op jit(solution)/shard_map/ppermute | solution.py:16
  126.1 21.3 %collective-permute-start.20 = (f32[4,6,1,128]{3,2,1,0:T(1,128)S(1)}, f32[4,6,1,128]{3,2,1,0:T(1,128)S(1)}, u32[]{:S(2)}, u32[]{:S(2)}) collective-permute-start(f32[4,6,1,128]{3,2,1,0:T(1,128)S(1)} %get-tuple-element.86), channel_id=1, source_target_pairs={{2,0},{3,1},{6,4},{7,5},{10,8},{11,9},{14,12},{15,13},{18,16},{19,... | collective-permute-start | bytes 36872 | tf_op jit(solution)/shard_map/ppermute | solution.py:17
  127.4 20.0 %collective-permute-start.21 = (f32[4,6,1,128]{3,2,1,0:T(1,128)S(1)}, f32[4,6,1,128]{3,2,1,0:T(1,128)S(1)}, u32[]{:S(2)}, u32[]{:S(2)}) collective-permute-start(f32[4,6,1,128]{3,2,1,0:T(1,128)S(1)} %get-tuple-element.85), channel_id=1, source_target_pairs={{0,2},{1,3},{4,6},{5,7},{8,10},{9,11},{12,14},{13,15},{16,18},{17,... | collective-permute-start | bytes 36872 | tf_op jit(solution)/shard_map/ppermute | solution.py:16
  148.0 4.5 %collective-permute-start.22 = (f32[4,6,34,1]{3,2,1,0:T(8,128)S(1)}, f32[4,6,34,1]{3,2,1,0:T(8,128)S(1)}, u32[]{:S(2)}, u32[]{:S(2)}) collective-permute-start(f32[4,6,34,1]{3,2,1,0:T(8,128)S(1)} %get-tuple-element.67), channel_id=1, source_target_pairs={{1,0},{3,2},{5,4},{7,6},{9,8},{11,10},{13,12},{15,14},{17,16},{19,... | collective-permute-start | bytes 9800 | tf_op jit(solution)/shard_map/ppermute | solution.py:17
  149.3 4.5 %collective-permute-start.23 = (f32[4,6,34,1]{3,2,1,0:T(8,128)S(1)}, f32[4,6,34,1]{3,2,1,0:T(8,128)S(1)}, u32[]{:S(2)}, u32[]{:S(2)}) collective-permute-start(f32[4,6,34,1]{3,2,1,0:T(8,128)S(1)} %get-tuple-element.68), channel_id=1, source_target_pairs={{0,1},{2,3},{4,5},{6,7},{8,9},{10,11},{12,13},{14,15},{16,17},{18,... | collective-permute-start | bytes 9800 | tf_op jit(solution)/shard_map/ppermute | solution.py:16
  181.0 11.8 %slice-start = ((f32[4,4,32,128]{3,2,1,0:T(8,128)}), f32[1,4,32,128]{3,2,1,0:T(8,128)S(1)}, s32[]{:S(2)}) async-start(f32[4,4,32,128]{3,2,1,0:T(8,128)} %copy-done), calls=%async_computation | async-start | bytes 131072 | tf_op jit(solution)/shard_map/slice | solution.py:194
  (13 other events, 44.6 us)
where the time goes:
time: 268 us; the launch traced here: 267 us
  other arithmetic  68.9 us (26%)
  starting transfers between devices  66.1 us (25%)
  blocking collectives  62.3 us (23%)
  local copies, waits for them, and re-layouts  55.9 us (21%)
  waiting for transfers between devices  10.9 us (4%)
  between operations  2.87 us (1%)
    psum x1, blocking collectives, per_device(): traces = lax.psum(jnp.stack(records), ('inline', 'xline', 'depth'))  62.3 us
    scatter-add x8, other arithmetic, deposit(): jnp.zeros((volume + 1,), jnp.float32).at[flat_index].add(values)[:volume]  61.4 us
    ppermute x12, starting transfers between devices, with_halo(): before = lax.ppermute(last, axis, up)  50.5 us
    gather x4, local copies, waits for them, and re-layouts, sample(): picked = field.reshape(-1)[jnp.minimum(flat_index, volume - 1)]  47.1 us
    ppermute x12, starting transfers between devices, with_halo(): after = lax.ppermute(initial, axis, down)  15.6 us
    ppermute x12, waiting for transfers between devices, with_halo(): before = lax.ppermute(last, axis, up)  8.96 us
  transfers between devices with their start and end apart: 24, of which 10 were waited for; matrix products, arithmetic and copies ran while one was open for 24% of the time, Pallas kernels for 0%

commit v1 on v0

v1 whole, which is shorter than its diff:
```python
import functools

import jax
import jax.numpy as jnp
from jax import lax
from jax.experimental import pallas as pl
from jax.experimental.pallas import tpu as pltpu
from jax.sharding import PartitionSpec as P

STEPS = 4
MESH = pl.DeviceIdType.MESH
AXES = ("inline", "xline", "depth")
LANES = 128
TOP = 8

DIRECTIONS = [
    (a, b, c)
    for a in (-1, 0, 1)
    for b in (-1, 0, 1)
    for c in (-1, 0, 1)
    if 1 <= abs(a) + abs(b) + abs(c) <= 2
]


def split_by(values, size):
    if size & (size - 1) == 0:
        return values >> (size.bit_length() - 1), values & (size - 1)
    quotient = lax.div(values, jnp.int32(size))
    return quotient, values - quotient * size


def three_parts(values):
    high = values.astype(jnp.bfloat16).astype(jnp.float32)
    rest = values - high
    middle = rest.astype(jnp.bfloat16).astype(jnp.float32)
    return high, middle, rest - middle


def kernel(
    sizes,
    forward_now,
    forward_before,
    adjoint_now,
    adjoint_before,
    courant,
    epsilon,
    delta,
    tilt_class,
    azimuth_class,
    tilt_table,
    azimuth_table,
    source_cell,
    wavelet,
    receiver_cells,
    receiver_data,
    forward_out,
    adjoint_out,
    image_out,
    traces_out,
    fields,
    model,
    classes,
    factors,
    zdiff,
    zsum,
    row_send,
    edge_send,
    row_got,
    depth_got,
    xy_got,
    xz_got,
    yz_got,
    hot_row,
    hot_lane,
    spread,
    terms,
    trace_own,
    trace_plane,
    trace_sum,
    trace_line,
    load_sem,
    halo_send,
    halo_recv,
    plane_send,
    plane_recv,
    line_send,
    line_recv,
):
    n_in, n_x, n_d = sizes
    _, cx, cy, cz = forward_now.shape
    nrec = receiver_cells.shape[1]
    groups = cy // 8
    here = tuple(lax.axis_index(axis) for axis in AXES)
    rows = slice(TOP, TOP + cy)

    def present(direction):
        ok = None
        for at, step, size in zip(here, direction, sizes):
            if step == 0:
                continue
            this = (at < size - 1) if step > 0 else (at > 0)
            ok = this if ok is None else jnp.logical_and(ok, this)
        return ok

    def target(direction):
        return {
            axis: at + step for axis, at, step in zip(AXES, here, direction) if step != 0
        }

    live = [d for d in DIRECTIONS if all(s == 0 or n > 1 for s, n in zip(d, sizes))]

    loads = []
    for number, (source, place) in enumerate(
        [
            (forward_now, fields.at[1, 0, :, pl.ds(1, cx), pl.ds(TOP, cy)]),
            (adjoint_now, fields.at[1, 1, :, pl.ds(1, cx), pl.ds(TOP, cy)]),
            (forward_before, fields.at[0, 0, :, pl.ds(1, cx), pl.ds(TOP, cy)]),
            (adjoint_before, fields.at[0, 1, :, pl.ds(1, cx), pl.ds(TOP, cy)]),
            (courant, model.at[0]),
            (epsilon, model.at[1]),
            (delta, model.at[2]),
            (tilt_class, classes.at[0]),
            (azimuth_class, classes.at[1]),
        ]
    ):
        load = pltpu.make_async_copy(source, place, load_sem.at[number])
        load.start()
        loads.append(load)

    barrier = pltpu.get_barrier_semaphore()

    def plane_peer(k):
        xline_at = lax.rem(here[1] + k // n_d, n_x)
        depth_at = lax.rem(here[2] + k % n_d, n_d)
        return {"xline": xline_at, "depth": depth_at}

    def line_peer(k):
        return {"inline": lax.rem(here[0] + k, n_in)}

    for k in range(1, n_x * n_d):
        pl.semaphore_signal(barrier, inc=1, device_id=plane_peer(k), device_id_type=MESH)
    for k in range(1, n_in):
        pl.semaphore_signal(barrier, inc=1, device_id=line_peer(k), device_id_type=MESH)
    crossing = [d for d in live if d[0] != 0 and (d[1] != 0 or d[2] != 0)]
    for d in crossing:

        @pl.when(present(d))
        def _(d=d):
            pl.semaphore_signal(barrier, inc=1, device_id=target(d), device_id_type=MESH)

    def got_ref(d, s, system):
        sides = [0 if step > 0 else 1 for step in d]
        if d[0] and not d[1] and not d[2]:
            plane = 0 if d[0] > 0 else cx + 1
            return fields.at[s + 1, system, :, plane, pl.ds(TOP, cy)]
        if d[1] and not d[0] and not d[2]:
            return row_got.at[s, system, sides[1]]
        if d[2] and not d[0] and not d[1]:
            return depth_got.at[s, system, sides[2]]
        if d[0] and d[1]:
            return xy_got.at[s, system, sides[0], sides[1]]
        if d[0] and d[2]:
            return xz_got.at[s, system, sides[0], sides[2]]
        return yz_got.at[s, system, sides[1], sides[2]]

    def clear(d):
        for s in range(STEPS):
            for system in range(2):
                place = got_ref(d, s, system)
                place[...] = jnp.zeros(place.shape, jnp.float32)

    for d in DIRECTIONS:
        if d not in live:
            clear(d)
        else:
            arrives = present(tuple(-step for step in d))

            @pl.when(jnp.logical_not(arrives))
            def _(d=d):
                clear(d)

    def sent_ref(d, s, system):
        if d[0] and not d[1] and not d[2]:
            plane = cx if d[0] > 0 else 1
            return fields.at[s + 1, system, :, plane, pl.ds(TOP, cy)]
        if d[2] and not d[0] and not d[1]:
            return fields.at[s + 1, system, :, pl.ds(1, cx), pl.ds(TOP, cy)]
        if d[1]:
            return row_send.at[s, system, 1 if d[1] > 0 else 0]
        return edge_send.at[s, system, 1 if d[0] > 0 else 0]

    def halo_copy(d, s, system):
        number = DIRECTIONS.index(d)
        return pltpu.make_async_remote_copy(
            src_ref=sent_ref(d, s, system),
            dst_ref=got_ref(d, s, system),
            send_sem=halo_send.at[s, system, number],
            recv_sem=halo_recv.at[s, system, number],
            device_id=target(d),
            device_id_type=MESH,
        )

    lane = lax.broadcasted_iota(jnp.int32, (8, LANES), 1)
    lane_plane = lax.broadcasted_iota(jnp.int32, (cy, LANES), 1)

    def stage(s, system):
        for side, plane in ((0, 1), (1, cx)):
            packed = jnp.zeros((8, LANES), jnp.float32)
            for f in range(2):
                for r in range(groups):
                    slot = f * groups + r
                    chunk = fields[s + 1, system, f, plane, TOP + 8 * r : TOP + 8 * r + 8, :]
                    packed = jnp.where(
                        lane == slot, pltpu.roll(chunk, (slot + 1) % LANES, 1), packed
                    )
                    other = 2 * groups + slot
                    packed = jnp.where(lane == other, pltpu.roll(chunk, other % LANES, 1), packed)
            edge_send[s, system, side] = packed
        for side, row in ((0, TOP), (1, TOP + cy - 1)):
            for f in range(2):
                for i in range(cx):
                    at = f * cx + i
                    row_send[s, system, side, at : at + 1, :] = fields[
                        s + 1, system, f, i + 1, row : row + 1, :
                    ]

    order = sorted(live, key=lambda d: (not (d[0] and not d[1] and not d[2]), d[0] == 0))

    def send(s, system):
        for d in order:

            @pl.when(present(d))
            def _(d=d):
                halo_copy(d, s, system).start()

    def receive(s, system):
        for d in order:

            @pl.when(present(tuple(-step for step in d)))
            def _(d=d):
                halo_copy(d, s, system).wait_recv()

    def drain(s, system):
        for d in order:

            @pl.when(present(d))
            def _(d=d):
                halo_copy(d, s, system).wait_send()

    def finish_halo(s, system):
        for side, row in ((0, TOP - 1), (1, TOP + cy)):
            tile = row_got[s, system, side]
            before = jnp.where(
                lax.broadcasted_iota(jnp.int32, tile.shape, 1) == LANES - 1,
                yz_got[s, system, side, 0],
                tile,
            )
            after = jnp.where(
                lax.broadcasted_iota(jnp.int32, tile.shape, 1) == 0,
                yz_got[s, system, side, 1],
                tile,
            )
            change = pltpu.roll(after, LANES - 1, 1) - pltpu.roll(before, 1, 1)
            for f in range(2):
                for i in range(cx):
                    at = f * cx + i
                    fields[s + 1, system, f, i + 1, row : row + 1, :] = tile[at : at + 1, :]
                    zdiff[f, i + 1, row : row + 1, :] = change[at : at + 1, :]
                for xside, plane, from_plane in ((0, 0, cx - 1), (1, cx + 1, 0)):
                    at = f * cx + from_plane
                    fields[s + 1, system, f, plane, row : row + 1, :] = xy_got[
                        s, system, xside, side, at : at + 1, :
                    ]
        for f in range(2):
            for i in range(cx):
                centre = fields[s + 1, system, f, i + 1, rows, :]
                before = jnp.where(
                    lane_plane == LANES - 1, depth_got[s, system, 0, f, i], centre
                )
                after = jnp.where(lane_plane == 0, depth_got[s, system, 1, f, i], centre)
                before = pltpu.roll(before, 1, 1)
                after = pltpu.roll(after, LANES - 1, 1)
                zdiff[f, i + 1, rows, :] = after - before
                zsum[f, i] = after + before
            for xside, plane in ((0, 0), (1, cx + 1)):
                low = xz_got[s, system, xside, 0]
                high = xz_got[s, system, xside, 1]
                for r in range(groups):
                    slot = f * groups + r
                    at = slice(TOP + 8 * r, TOP + 8 * r + 8)
                    chunk = fields[s + 1, system, f, plane, at, :]
                    before = jnp.where(
                        lane == 0,
                        pltpu.roll(low, (-slot) % LANES, 1),
                        pltpu.roll(chunk, 1, 1),
                    )
                    after = jnp.where(
                        lane == LANES - 1,
                        pltpu.roll(high, (LANES - 1 - 2 * groups - slot) % LANES, 1),
                        pltpu.roll(chunk, LANES - 1, 1),
                    )
                    zdiff[f, plane, at, :] = after - before

    up = slice(TOP - 1, TOP + cy - 1)
    down = slice(TOP + 1, TOP + cy + 1)

    def advance(s, system):
        for i in range(cx):
            axial = []
            lap = None
            for f in range(2):
                now = fields.at[s + 1, system, f]
                centre = now[i + 1, rows, :]
                twice = 2.0 * centre
                dxx = now[i + 2, rows, :] + now[i, rows, :] - twice
                dyy = now[i + 1, down, :] + now[i + 1, up, :] - twice
                dzz = zsum[f, i] - twice
                dxy = (
                    now[i + 2, down, :]
                    - now[i + 2, up, :]
                    - now[i, down, :]
                    + now[i, up, :]
                )
                dxz = zdiff[f, i + 2, rows, :] - zdiff[f, i, rows, :]
                dyz = zdiff[f, i + 1, down, :] - zdiff[f, i + 1, up, :]
                axial.append(
                    factors[3, i] * dxx
                    + factors[4, i] * dyy
                    + factors[5, i] * dzz
                    + factors[6, i] * dxy
                    + factors[7, i] * dxz
                    + factors[8, i] * dyz
                )
                if f == 0:
                    lap = dxx + dyy + dzz
            plane_part = lap - axial[0]
            along = factors[2, i] * axial[1]
            if system == 0:
                row_at = lax.broadcasted_iota(jnp.int32, (cy, LANES), 0)
                cell = (
                    (here[0] * cx + i) * (n_x * cy) + here[1] * cy + row_at
                ) * (n_d * cz) + here[2] * cz + lane_plane
                added = jnp.where(cell == source_cell[0], wavelet[s], 0.0)
            else:
                added = terms[s, i]
            new = []
            for f in range(2):
                value = (
                    2.0 * fields[s + 1, system, f, i + 1, rows, :]
                    - fields[s, system, f, i + 1, rows, :]
                    + factors[f, i] * plane_part
                    + along
                    + added
                )
                fields[s + 2, system, f, i + 1, rows, :] = value
                new.append(value)
            if system == 1:
                product = (
                    fields[s + 2, 0, 0, i + 1, rows, :] * new[0]
                    + fields[s + 2, 0, 1, i + 1, rows, :] * new[1]
                )
                if s == 0:
                    image_out[i] = product
                else:
                    image_out[i] = image_out[i] + product
            if s == STEPS - 1:
                out = forward_out if system == 0 else adjoint_out
                out[0, i] = new[0]
                out[1, i] = new[1]

    def coefficients():
        tilt_sine, tilt_cosine = jnp.sin(tilt_table[...]), jnp.cos(tilt_table[...])
        turn_sine, turn_cosine = jnp.sin(azimuth_table[...]), jnp.cos(azimuth_table[...])

        def look(which, i, tables):
            chosen = classes[which, i]
            found = [jnp.zeros((cy, LANES), jnp.float32) for _ in tables]
            for k in range(tables[0].shape[1]):
                match = chosen == k
                found = [
                    jnp.where(match, jnp.broadcast_to(t[:, k : k + 1], (cy, LANES)), v)
                    for t, v in zip(tables, found)
                ]
            return found

        for i in range(cx):
            sine, third = look(0, i, (tilt_sine, tilt_cosine))
            turned, across = look(1, i, (turn_cosine, turn_sine))
            first, second = sine * turned, sine * across
            base = model[0, i]
            factors[0, i] = base * (1.0 + 2.0 * model[1, i])
            factors[1, i] = base * (1.0 + 2.0 * model[2, i])
            factors[2, i] = base
            factors[3, i] = first * first
            factors[4, i] = second * second
            factors[5, i] = third * third
            factors[6, i] = 0.5 * first * second
            factors[7, i] = 0.5 * first * third
            factors[8, i] = 0.5 * second * third

    def receivers():
        cells = receiver_cells[...]
        upper, depth_at = split_by(cells, n_d * cz)
        inline_at, xline_at = split_by(upper, n_x * cy)
        inline_at = inline_at - here[0] * cx
        xline_at = xline_at - here[1] * cy
        depth_at = depth_at - here[2] * cz
        inside = (
            (inline_at >= 0)
            & (inline_at < cx)
            & (xline_at >= 0)
            & (xline_at < cy)
            & (depth_at >= 0)
            & (depth_at < cz)
        )
        row_of = jnp.where(inside, inline_at * cy + xline_at, -1)
        lane_of = jnp.where(inside, depth_at, -1)
        row_match = (
            lax.broadcasted_iota(jnp.int32, (cx * cy, nrec), 0)
            == jnp.broadcast_to(row_of, (cx * cy, nrec))
        )
        lane_match = (
            lax.broadcasted_iota(jnp.int32, (cz, nrec), 0)
            == jnp.broadcast_to(lane_of, (cz, nrec))
        )
        hot_row[...] = jnp.where(row_match, 1.0, 0.0)
        lanes_hot = jnp.where(lane_match, 1.0, 0.0).astype(jnp.bfloat16)
        for part in range(3):
            hot_lane[part * cz : (part + 1) * cz, :] = lanes_hot
        parts = three_parts(receiver_data[...])
        volume = cx * cy
        for s in range(STEPS):
            for number, part in enumerate(parts):
                start = (s * 3 + number) * volume
                spread[start : start + volume, :] = (
                    hot_row[...] * jnp.broadcast_to(part[s : s + 1, :], (volume, nrec))
                ).astype(jnp.bfloat16)
            got = lax.dot_general(
                spread[s * 3 * volume : (s + 1) * 3 * volume, :],
                hot_lane[0:cz, :],
                (((1,), (1,)), ((), ())),
                preferred_element_type=jnp.float32,
            )
            total = got[:volume] + got[volume : 2 * volume] + got[2 * volume :]
            for i in range(cx):
                terms[s, i] = total[i * cy : (i + 1) * cy, :]

    def sample(s):
        planes = [fields[s + 2, 0, 0, i + 1, rows, :] for i in range(cx)]
        field = jnp.concatenate(planes, axis=0)
        parts = jnp.concatenate([p.astype(jnp.bfloat16) for p in three_parts(field)], axis=1)
        picked = jnp.dot(parts, hot_lane[...], preferred_element_type=jnp.float32)
        trace_own[s] = jnp.sum(picked * hot_row[...], axis=0, keepdims=True)

    def plane_copy(s, k):
        return pltpu.make_async_remote_copy(
            src_ref=trace_own.at[s],
            dst_ref=trace_plane.at[s, k],
            send_sem=plane_send.at[s, k],
            recv_sem=plane_recv.at[s, k],
            device_id=plane_peer(k),
            device_id_type=MESH,
        )

    def line_copy(s, k):
        return pltpu.make_async_remote_copy(
            src_ref=trace_sum.at[s],
            dst_ref=trace_line.at[s, k],
            send_sem=line_send.at[s, k],
            recv_sem=line_recv.at[s, k],
            device_id=line_peer(k),
            device_id_type=MESH,
        )

    def share_plane(s):
        for k in range(1, n_x * n_d):
            plane_copy(s, k).start()

    def share_line(s):
        total = trace_own[s]
        for k in range(1, n_x * n_d):
            plane_copy(s, k).wait_recv()
            total = total + trace_plane[s, k]
        trace_sum[s] = total
        for k in range(1, n_in):
            line_copy(s, k).start()

    def finish_trace(s):
        total = trace_sum[s]
        for k in range(1, n_in):
            line_copy(s, k).wait_recv()
            total = total + trace_line[s, k]
        traces_out[s : s + 1, :] = total

    expected = jnp.int32(n_x * n_d - 1 + n_in - 1)
    for d in crossing:
        expected = expected + jnp.where(present(d), 1, 0)
    loads[0].wait()
    stage(0, 0)
    loads[1].wait()
    stage(0, 1)
    pl.semaphore_wait(barrier, expected)
    send(0, 0)
    send(0, 1)
    for load in loads[2:]:
        load.wait()
    coefficients()
    receivers()
    for s in range(STEPS):
        for system in range(2):
            receive(s, system)
            finish_halo(s, system)
            advance(s, system)
            if s < STEPS - 1:
                stage(s + 1, system)
                send(s + 1, system)
        sample(s)
        share_plane(s)
        if s > 0:
            share_line(s - 1)
    share_line(STEPS - 1)
    for s in range(STEPS):
        finish_trace(s)
    for s in range(STEPS):
        for system in range(2):
            drain(s, system)
        for k in range(1, n_x * n_d):
            plane_copy(s, k).wait_send()
        for k in range(1, n_in):
            line_copy(s, k).wait_send()


def per_device(sizes, *operands):
    shapes = [operand.shape for operand in operands]
    _, cx, cy, cz = shapes[0]
    nrec = shapes[13][0]
    n_in, n_x, n_d = sizes
    operands = list(operands)
    for which in (9, 10, 13):
        operands[which] = operands[which].reshape(1, -1)
    f32, bf16 = jnp.float32, jnp.bfloat16
    padded = cy + 2 * TOP
    combos = 2 * cx
    scratch = [
        pltpu.VMEM((STEPS + 2, 2, 2, cx + 2, padded, cz), f32),
        pltpu.VMEM((3, cx, cy, cz), f32),
        pltpu.VMEM((2, cx, cy, cz), jnp.int32),
        pltpu.VMEM((9, cx, cy, cz), f32),
        pltpu.VMEM((2, cx + 2, padded, cz), f32),
        pltpu.VMEM((2, cx, cy, cz), f32),
        pltpu.VMEM((STEPS, 2, 2, combos, cz), f32),
        pltpu.VMEM((STEPS, 2, 2, 8, cz), f32),
        pltpu.VMEM((STEPS, 2, 2, combos, cz), f32),
        pltpu.VMEM((STEPS, 2, 2, 2, cx, cy, cz), f32),
        pltpu.VMEM((STEPS, 2, 2, 2, combos, cz), f32),
        pltpu.VMEM((STEPS, 2, 2, 2, 8, cz), f32),
        pltpu.VMEM((STEPS, 2, 2, 2, combos, cz), f32),
        pltpu.VMEM((cx * cy, nrec), f32),
        pltpu.VMEM((3 * cz, nrec), bf16),
        pltpu.VMEM((3 * STEPS * cx * cy, nrec), bf16),
        pltpu.VMEM((STEPS, cx, cy, cz), f32),
        pltpu.VMEM((STEPS, 1, nrec), f32),
        pltpu.VMEM((STEPS, n_x * n_d, 1, nrec), f32),
        pltpu.VMEM((STEPS, 1, nrec), f32),
        pltpu.VMEM((STEPS, n_in, 1, nrec), f32),
        pltpu.SemaphoreType.DMA((9,)),
        pltpu.SemaphoreType.DMA((STEPS, 2, len(DIRECTIONS))),
        pltpu.SemaphoreType.DMA((STEPS, 2, len(DIRECTIONS))),
        pltpu.SemaphoreType.DMA((STEPS, n_x * n_d)),
        pltpu.SemaphoreType.DMA((STEPS, n_x * n_d)),
        pltpu.SemaphoreType.DMA((STEPS, n_in)),
        pltpu.SemaphoreType.DMA((STEPS, n_in)),
    ]
    vmem = pl.BlockSpec(memory_space=pltpu.VMEM)
    smem = pl.BlockSpec(memory_space=pltpu.SMEM)
    anywhere = pl.BlockSpec(memory_space=pl.ANY)
    return pl.pallas_call(
        functools.partial(kernel, sizes),
        out_shape=(
            jax.ShapeDtypeStruct((2, cx, cy, cz), f32),
            jax.ShapeDtypeStruct((2, cx, cy, cz), f32),
            jax.ShapeDtypeStruct((cx, cy, cz), f32),
            jax.ShapeDtypeStruct((STEPS, nrec), f32),
        ),
        in_specs=[anywhere] * 9 + [vmem, vmem, smem, smem, vmem, vmem],
        out_specs=(vmem, vmem, vmem, vmem),
        scratch_shapes=scratch,
        compiler_params=pltpu.CompilerParams(
            collective_id=0, has_side_effects=True, vmem_limit_bytes=56 * 2**20
        ),
        name="wavefields",
    )(*operands)


def solution(mesh):
    sizes = tuple(mesh.shape[axis] for axis in AXES)
    field = P(None, ("shot", "inline"), "xline", "depth")
    cell = P("inline", "xline", "depth")
    return jax.shard_map(
        functools.partial(per_device, sizes),
        mesh=mesh,
        in_specs=(
            field, field, field, field,
            cell, cell, cell, cell, cell,
            P(), P(), P("shot"), P("shot"), P("shot"), P(None, "shot"),
        ),
        out_specs=(field, field, P(("shot", "inline"), "xline", "depth"), P(None, "shot")),
        check_vma=False,
    )
```

time: 268 us -> 38.3 us (0.14)
  other arithmetic: 68.9 us -> 0 us
  starting transfers between devices: 66.1 us -> 0 us
  blocking collectives: 62.3 us -> 0 us
  local copies, waits for them, and re-layouts: 55.9 us -> 3.84 us
  Pallas kernels: 0 us -> 32.8 us
  waiting for transfers between devices: 10.9 us -> 0 us
    ppermute x24 -> x0, starting transfers between devices: 66.1 us -> none  [the longest x12 50.5 us: with_halo(): before = lax.ppermute(last, axis, up)]
    psum x1 -> x0, blocking collectives: 62.3 us -> none  [per_device(): traces = lax.psum(jnp.stack(records), ('inline', 'xline', 'depth'))]
    scatter-add x8 -> x0, other arithmetic: 61.4 us -> none  [deposit(): jnp.zeros((volume + 1,), jnp.float32).at[flat_index].add(values)[:volume]]
    gather x4 -> x0, local copies, waits for them, and re-layouts: 47.1 us -> none  [sample(): picked = field.reshape(-1)[jnp.minimum(flat_index, volume - 1)]]
    pallas_call x0 -> x1, Pallas kernels: none -> 32.8 us  [per_device(): pl.pallas_call(functools.partial(kernel, sizes), out_shape=(jax.ShapeDtyp...]
    ppermute x24 -> x0, waiting for transfers between devices: 10.9 us -> none  [the longest x12 8.96 us: with_halo(): before = lax.ppermute(last, axis, up)]
    slice x31 -> x0, local copies, waits for them, and re-layouts: 4.47 us -> none  [the longest x12 2.76 us: deposit(): jnp.zeros((volume + 1,), jnp.float32).at[flat_index].add(values)[:volume]]
    add x16 -> x0, other arithmetic: 3.49 us -> none  [the longest x4 2.21 us: advance(): factors[3] * inline_inline + factors[4] * xline_xline]
  transfers between devices with their start and end apart: 24 -> 0, of which waited for: 10 -> 0; matrix products, arithmetic and copies ran while one was open for 24% -> 0% of each run, Pallas kernels for 0% -> 0%
where the time goes in v1:
time: 38.3 us; the launch traced here: 38 us
  Pallas kernels  32.8 us (86%)
  local copies, waits for them, and re-layouts  3.84 us (10%)
  between operations  1.3 us (3%)
    pallas_call x1, Pallas kernels, per_device(): pl.pallas_call(functools.partial(kernel, sizes), out_shape=(jax.ShapeDtyp...  32.8 us
    unnamed x10, local copies, waits for them, and re-layouts  3.84 us

profile of v1, /device:TPU:0, one launch (start us, length us, event | category | flops | bytes accessed | tf_op | source)
XLA Modules:
  0.0 38.0 jit_solution(7162471918530609046)
XLA Ops:
  1.3 32.8 %wavefields.1 = (f32[2,4,32,128]{3,2,1,0:T(8,128)}, f32[2,4,32,128]{3,2,1,0:T(8,128)}, f32[4,32,128]{2,1,0:T(8,128)}, f32[4,2048]{1,0:T(4,128)}) custom-call(f32[2,4,32,128]{3,2,1,0:T(8,128)} %forward_now.1, f32[2,4,32,128]{3,2,1,0:T(8,128)} %forward_before.1, f32[2,4,32,128]{3,2,1,0:T(8,128)} %adjoint_now.1, f32[2,4,32,128]{3,2,1,0:T(8,128)} %adjoint_before.1, ...), custom_call_target="tpu_custom_call" | custom-call | tf_op jit(solution)/shard_map/wavefields/pallas_call | solution.py:577
  34.1 0.0 copy-start
  34.1 1.6 %copy.24 = f32[2,4,32,128]{3,2,1,0:T(8,128)} copy(f32[2,4,32,128]{3,2,1,0:T(8,128)} %get-tuple-element.8) | data formatting | bytes 262144
  35.7 0.0 copy-done
  35.7 0.0 copy-start.1
  35.8 0.7 %copy.25 = f32[2,4,32,128]{3,2,1,0:T(8,128)} copy(f32[2,4,32,128]{3,2,1,0:T(8,128)S(1)} %copy-done) | data formatting | bytes 262144
  36.4 0.2 copy-done.1
  36.6 0.0 copy-start.2
  36.6 0.6 %copy.26 = f32[4,32,128]{2,1,0:T(8,128)} copy(f32[4,32,128]{2,1,0:T(8,128)S(1)} %copy-done.1) | data formatting | bytes 131072
  37.2 0.1 copy-done.2
  37.4 0.6 %copy.27 = f32[4,2048]{1,0:T(4,128)} copy(f32[4,2048]{1,0:T(4,128)S(1)} %copy-done.2) | data formatting | bytes 65536
Async XLA Ops:
  34.1 1.6 %copy-start = (f32[2,4,32,128]{3,2,1,0:T(8,128)S(1)}, f32[2,4,32,128]{3,2,1,0:T(8,128)}, u32[]{:S(2)}) copy-start(f32[2,4,32,128]{3,2,1,0:T(8,128)} %get-tuple-element.9) | copy-start | bytes 393220
  35.7 0.9 %copy-start.1 = (f32[4,32,128]{2,1,0:T(8,128)S(1)}, f32[4,32,128]{2,1,0:T(8,128)}, u32[]{:S(2)}) copy-start(f32[4,32,128]{2,1,0:T(8,128)} %get-tuple-element.10) | copy-start | bytes 196612
  36.6 0.8 %copy-start.2 = (f32[4,2048]{1,0:T(4,128)S(1)}, f32[4,2048]{1,0:T(4,128)}, u32[]{:S(2)}) copy-start(f32[4,2048]{1,0:T(4,128)} %get-tuple-element.11) | copy-start | bytes 98308

commit v2 on v1

--- a/solution.py
+++ b/solution.py
@@ -64,6 +64,7 @@
     zdiff,
     zsum,
     row_send,
+    row_edge,
     edge_send,
     row_got,
     depth_got,
@@ -185,6 +186,8 @@
             return fields.at[s + 1, system, :, plane, pl.ds(TOP, cy)]
         if d[2] and not d[0] and not d[1]:
             return fields.at[s + 1, system, :, pl.ds(1, cx), pl.ds(TOP, cy)]
+        if d[0] and d[1]:
+            return row_edge.at[s, system, 1 if d[1] > 0 else 0]
         if d[1]:
             return row_send.at[s, system, 1 if d[1] > 0 else 0]
         return edge_send.at[s, system, 1 if d[0] > 0 else 0]
@@ -203,7 +206,7 @@
     lane = lax.broadcasted_iota(jnp.int32, (8, LANES), 1)
     lane_plane = lax.broadcasted_iota(jnp.int32, (cy, LANES), 1)
 
-    def stage(s, system):
+    def stage_edges(s, system):
         for side, plane in ((0, 1), (1, cx)):
             packed = jnp.zeros((8, LANES), jnp.float32)
             for f in range(2):
@@ -217,6 +220,16 @@
                     packed = jnp.where(lane == other, pltpu.roll(chunk, other % LANES, 1), packed)
             edge_send[s, system, side] = packed
         for side, row in ((0, TOP), (1, TOP + cy - 1)):
+            row_edge[s, system, side] = jnp.zeros(row_edge.shape[3:], jnp.float32)
+            for f in range(2):
+                for i in sorted({0, cx - 1}):
+                    at = f * cx + i
+                    row_edge[s, system, side, at : at + 1, :] = fields[
+                        s + 1, system, f, i + 1, row : row + 1, :
+                    ]
+
+    def stage_rows(s, system):
+        for side, row in ((0, TOP), (1, TOP + cy - 1)):
             for f in range(2):
                 for i in range(cx):
                     at = f * cx + i
@@ -225,9 +238,11 @@
                     ]
 
     order = sorted(live, key=lambda d: (not (d[0] and not d[1] and not d[2]), d[0] == 0))
-
-    def send(s, system):
-        for d in order:
+    early = [d for d in order if d[0] != 0]
+    late = [d for d in order if d[0] == 0]
+
+    def send(s, system, which):
+        for d in which:
 
             @pl.when(present(d))
             def _(d=d):
@@ -304,8 +319,11 @@
     up = slice(TOP - 1, TOP + cy - 1)
     down = slice(TOP + 1, TOP + cy + 1)
 
-    def advance(s, system):
-        for i in range(cx):
+    outer = sorted({0, cx - 1})
+    inner = [i for i in range(cx) if i not in outer]
+
+    def advance(s, system, planes):
+        for i in planes:
             axial = []
             lap = None
             for f in range(2):
@@ -496,12 +514,15 @@
     for d in crossing:
         expected = expected + jnp.where(present(d), 1, 0)
     loads[0].wait()
-    stage(0, 0)
+    stage_edges(0, 0)
+    stage_rows(0, 0)
     loads[1].wait()
-    stage(0, 1)
+    stage_edges(0, 1)
+    stage_rows(0, 1)
     pl.semaphore_wait(barrier, expected)
-    send(0, 0)
-    send(0, 1)
+    for system in range(2):
+        send(0, system, early)
+        send(0, system, late)
     for load in loads[2:]:
         load.wait()
     coefficients()
@@ -510,14 +531,23 @@
         for system in range(2):
             receive(s, system)
             finish_halo(s, system)
-            advance(s, system)
+            advance(s, system, outer)
             if s < STEPS - 1:
-                stage(s + 1, system)
-                send(s + 1, system)
-        sample(s)
-        share_plane(s)
-        if s > 0:
-            share_line(s - 1)
+                stage_edges(s + 1, system)
+                send(s + 1, system, early)
+            advance(s, system, inner)
+            if s < STEPS - 1:
+                stage_rows(s + 1, system)
+                send(s + 1, system, late)
+            elif system == 0:
+                sample(s)
+                share_plane(s)
+                share_line(s - 1)
+        if s < STEPS - 1:
+            sample(s)
+            share_plane(s)
+            if s > 0:
+                share_line(s - 1)
     share_line(STEPS - 1)
     for s in range(STEPS):
         finish_trace(s)
@@ -528,6 +558,12 @@
             plane_copy(s, k).wait_send()
         for k in range(1, n_in):
             line_copy(s, k).wait_send()
+
+
+def publish(*refs):
+    half = len(refs) // 2
+    for source, place in zip(refs[:half], refs[half:]):
+        place[...] = source[...]
 
 
 def per_device(sizes, *operands):
@@ -548,6 +584,7 @@
         pltpu.VMEM((9, cx, cy, cz), f32),
         pltpu.VMEM((2, cx + 2, padded, cz), f32),
         pltpu.VMEM((2, cx, cy, cz), f32),
+        pltpu.VMEM((STEPS, 2, 2, combos, cz), f32),
         pltpu.VMEM((STEPS, 2, 2, combos, cz), f32),
         pltpu.VMEM((STEPS, 2, 2, 8, cz), f32),
         pltpu.VMEM((STEPS, 2, 2, combos, cz), f32),
@@ -574,7 +611,7 @@
     vmem = pl.BlockSpec(memory_space=pltpu.VMEM)
     smem = pl.BlockSpec(memory_space=pltpu.SMEM)
     anywhere = pl.BlockSpec(memory_space=pl.ANY)
-    return pl.pallas_call(
+    made = pl.pallas_call(
         functools.partial(kernel, sizes),
         out_shape=(
             jax.ShapeDtypeStruct((2, cx, cy, cz), f32),
@@ -590,6 +627,13 @@
         ),
         name="wavefields",
     )(*operands)
+    return pl.pallas_call(
+        publish,
+        out_shape=[jax.ShapeDtypeStruct(m.shape, m.dtype) for m in made],
+        in_specs=[vmem] * len(made),
+        out_specs=[vmem] * len(made),
+        name="publish",
+    )(*made)
 
 
 def solution(mesh):

time: 38.3 us -> 35.5 us (0.927)
  local copies, waits for them, and re-layouts: 3.84 us -> 0 us
  Pallas kernels: 32.8 us -> 34 us
    unnamed x10 -> x0, local copies, waits for them, and re-layouts: 3.84 us -> none
    pallas_call x0 -> x1, Pallas kernels: none -> 1.71 us  [per_device(): pl.pallas_call(publish, out_shape=[jax.ShapeDtypeStruct(m.shape, m.dtype)...]
    pallas_call x1, Pallas kernels: 32.8 us -> 32.3 us  [per_device(): pl.pallas_call(functools.partial(kernel, sizes), out_shape=(jax.ShapeDtyp...]
where the time goes in v2:
time: 35.5 us; the launch traced here: 35.3 us
  Pallas kernels  34 us (96%)
  between operations  1.29 us (4%)
    pallas_call x1, Pallas kernels, per_device(): pl.pallas_call(functools.partial(kernel, sizes), out_shape=(jax.ShapeDtyp...  32.3 us
    pallas_call x1, Pallas kernels, per_device(): pl.pallas_call(publish, out_shape=[jax.ShapeDtypeStruct(m.shape, m.dtype)...  1.71 us

profile of v2, /device:TPU:0, one launch (start us, length us, event | category | flops | bytes accessed | tf_op | source)
XLA Modules:
  0.0 35.3 jit_solution(14642933046694766874)
XLA Ops:
  1.3 32.3 %wavefields.1 = (f32[2,4,32,128]{3,2,1,0:T(8,128)}, f32[2,4,32,128]{3,2,1,0:T(8,128)}, f32[4,32,128]{2,1,0:T(8,128)}, f32[4,2048]{1,0:T(4,128)}) custom-call(f32[2,4,32,128]{3,2,1,0:T(8,128)} %forward_now.1, f32[2,4,32,128]{3,2,1,0:T(8,128)} %forward_before.1, f32[2,4,32,128]{3,2,1,0:T(8,128)} %adjoint_now.1, f32[2,4,32,128]{3,2,1,0:T(8,128)} %adjoint_before.1, ...), custom_call_target="tpu_custom_call" | custom-call | tf_op jit(solution)/shard_map/wavefields/pallas_call | solution.py:614
  33.6 1.7 %publish.1 = (f32[2,4,32,128]{3,2,1,0:T(8,128)}, f32[2,4,32,128]{3,2,1,0:T(8,128)}, f32[4,32,128]{2,1,0:T(8,128)}, f32[4,2048]{1,0:T(4,128)}) custom-call(f32[2,4,32,128]{3,2,1,0:T(8,128)} %get-tuple-element.8.refs_0_, f32[2,4,32,128]{3,2,1,0:T(8,128)} %get-tuple-element.9.refs_1_, f32[4,32,128]{2,1,0:T(8,128)} %get-tuple-element.10.refs_2_, ...), custom_call_target="tpu_custom_call" | custom-call | tf_op jit(solution)/shard_map/publish/pallas_call | solution.py:630
